TPU v7x, 128 devices: a whole 4x4x4 slice. The times are simulated.
128 devices in a mesh: heads: 1, cp: 128 (over z, y, x, core).
Axes of the slice: x: 4, y: 4, z: 4, core: 2. Of those that a mesh axis runs over, the one named last changes fastest.
Arguments:
- query: bfloat16 [2, 2048, 32, 128], P(None, 'cp', 'heads')
- attn_out: bfloat16 [2, 2048, 32, 128], P(None, 'cp', 'heads')
- grad_out: bfloat16 [2, 2048, 32, 128], P(None, 'cp', 'heads')
- row_lse: float32 [2, 2048, 32], P(None, 'cp', 'heads')
- key_cache: bfloat16 [12288, 8, 128], P('cp', 'heads')
- value_cache: bfloat16 [12288, 8, 128], P('cp', 'heads')
Outputs:
- output 1: bfloat16 [2, 2048, 32, 128], P(None, 'cp', 'heads')
- output 2: float32 [12288, 8, 128], P('cp', 'heads')
- output 3: float32 [12288, 8, 128], P('cp', 'heads')
All inputs are finite; a program needn't handle non-finite values.
Results may differ from a plain program's by a relative error of at most 0.00468.
Values are sent between devices in bfloat16 or wider.
A program may use at most 1 GiB of HBM per device.

v0:
```python
import functools

import jax
import jax.numpy as jnp
from jax import lax
from jax.experimental import pallas as pl
from jax.experimental.pallas import tpu as pltpu
from jax.sharding import PartitionSpec as P

F32 = jnp.float32
BF16 = jnp.bfloat16
MESH = pl.DeviceIdType.MESH
LOG2E = 1.4426950408889634
Z = 4
HD = 128
PQ = 1024
PK = 768
TK = 256


QUERIES = "0101230123012332"
KEYS = "0011113333222200"
FORWARD_Q = ".23............."
FORWARD_K = "...32..........."
ARRIVE_Q = ".1..23.........."
ARRIVE_K = "..1...3...2....."
KC = "...........1..3."
QC = "..............01"
KB = "........1...3..2"
QB = "............01.."
QA = "..........01..32"
KA = ".....1...3...2.0"


def kernel(shape, msg, ld, dq_out, dk_out, dv_out, qd, kv, kn, ldg, qt, kt, lb, db,
           dq, acc, part, rak, rbk, raq, rbq, outk, outq,
           a_send, a_q, a_k, a_l, f_send, q_r, k_r, l_r,
           ka, kb, qa, qb, p_send, o_send, o_r):
    n_slices, rows_dev, keys_dev, head_dim, cp_size = shape
    slice_len = rows_dev * cp_size
    prefix0 = keys_dev * cp_size - n_slices * slice_len
    inv_sqrt = head_dim ** -0.5
    c2 = inv_sqrt * LOG2E
    me = lax.axis_index("cp")
    core = lax.rem(me, 2)
    xi = lax.rem(me // 2, 4)
    yi = lax.rem(me // 8, 4)
    zi = me // 32
    head = zi * 2 + core
    first = core == 0
    gq, gk = jnp.where(first, xi, yi), jnp.where(first, yi, xi)
    sq, sk = jnp.where(first, 2, 8), jnp.where(first, 8, 2)
    kbase, kstep = jnp.where(first, xi * 192, yi * PK), jnp.where(first, 576, 0)
    qbase, qstep = jnp.where(first, yi * 128, xi * 32), jnp.where(first, 0, 96)

    def ring(i, d):
        return lax.rem(i + d + 4, 4)

    qP, qM, qO = ring(gq, 1), ring(gq, -1), ring(gq, 2)
    kP, kM, kO = ring(gk, 1), ring(gk, -1), ring(gk, 2)
    dqp, dqm, dqo = me + (qP - gq) * sq, me + (qM - gq) * sq, me + (qO - gq) * sq
    dkp, dkm, dko = me + (kP - gk) * sk, me + (kM - gk) * sk, me + (kO - gk) * sk

    def dev_z(z, c):
        return z * 32 + yi * 8 + xi * 2 + c

    def off(a):
        return a ^ (a >> 1)

    def piece_z(a):
        return ring(zi, -off(a))

    def rcopy(src, dst, ss, rs, to):
        return pltpu.make_async_remote_copy(src_ref=src, dst_ref=dst, send_sem=ss, recv_sem=rs,
                                            device_id={"cp": to}, device_id_type=MESH)

    barrier = pltpu.get_barrier_semaphore()
    peers = [dqp, dqm, dqo, dkp, dkm, dko]
    for o in range(4):
        for dc in range(2):
            if o or dc:
                peers.append(dev_z(ring(zi, o), core ^ dc))
    for p in peers:
        pl.semaphore_signal(barrier, inc=1, device_id={"cp": p}, device_id_type=MESH)
    pl.semaphore_wait(barrier, len(peers))

    def got(ref, sem):
        rcopy(ref, ref, p_send.at[0], sem, me).wait_recv()

    def sent(ref, sem):
        rcopy(ref, ref, sem, l_r.at[0], me).wait_send()

    def to_head(a, dc):
        tz, tc = ring(zi, off(a)), core ^ dc
        tq, tk = jnp.where(tc == 0, xi, yi), jnp.where(tc == 0, yi, xi)
        return tz * 2 + tc, dev_z(tz, tc), tq, tk

    def q_msg(h):
        return msg.at[h, pl.ds(0, 256)].reshape(2, 2, 64, HD)

    def k_msg(h):
        return msg.at[h, pl.ds(256, 192)].reshape(2, 96, HD)

    def a2a_q(a, dc):
        h, to, tq, _ = to_head(a, dc)
        rcopy(q_msg(h), qd.at[zi, :, :, tq, core], a_send.at[0], a_q.at[a, dc], to).start()
        rcopy(ld.at[h], ldg.at[zi, tq, core], a_send.at[2], a_l.at[a], to).start()

    def a2a_k(a, dc):
        h, to, _, tk = to_head(a, dc)
        rcopy(k_msg(h), kv.at[zi, :, tk, core], a_send.at[1], a_k.at[a, dc], to).start()

    a2a_q(0, 1)
    a2a_k(0, 1)
    for f in (a2a_q, a2a_k):
        for dc in (1, 0):
            for a in (1, 2):
                f(a, dc)

    qd[zi, :, :, gq, core] = msg[head, 0:256].reshape(2, 2, 64, HD)
    kv[zi, :, gk, core] = msg[head, 256:448].reshape(2, 96, HD)
    ldg[zi, gq, core] = ld[head]

    def forward_q(a, dc):
        sz, sc = piece_z(a), core ^ dc
        c = qd.at[sz, :, :, gq, sc]
        if not (isinstance(a, int) and a == 0 and dc == 0):
            got(c, a_q.at[a, dc])
        for to in (dqp, dqm, dqo):
            rcopy(c, c, f_send.at[0], q_r.at[a], to).start()

    def forward_k(a, dc, wait=True):
        sz, sc = piece_z(a), core ^ dc
        c = kv.at[sz, :, gk, sc]
        if not (isinstance(a, int) and a == 0 and dc == 0) and wait:
            got(c, a_k.at[a, dc])
        for to in (dkp, dkm, dko):
            rcopy(c, c, f_send.at[1], k_r.at[a], to).start()

    def forward_ld(a):
        c = ldg.at[piece_z(a), gq]
        got(c.at[0] if isinstance(a, int) and a == 0 else c, a_l.at[a])
        for to in (dqp, dqm, dqo):
            rcopy(c, c, f_send.at[2], l_r.at[a], to).start()

    def arrive_q(a):
        sz = piece_z(a)
        got(qd.at[sz, :, :, 0:3], q_r.at[a])
        got(ldg.at[sz, 0:3], l_r.at[a])
        for b in range(2):
            qt[sz, b] = qd[sz, b].reshape(PQ, 128).T
        for x in range(4):
            for c in range(2):
                for ref, r in ((lb, 0), (db, 1)):
                    t = jnp.broadcast_to(ldg[sz, x, c, r:r + 1, :], (128, 128)).T
                    ref[sz, 0, x, pl.ds(c * 64, 64)] = t[:64]
                    ref[sz, 1, x, pl.ds(c * 64, 64)] = t[64:]

    def arrive_k(a):
        sz = piece_z(a)
        got(kv.at[sz, :, 0:3], k_r.at[a])
        for b in range(2):
            kt[sz, b] = kv[sz, b].reshape(PK, 128).T
        kn[sz] = kv[sz, 0].reshape(PK, 128)

    for dc in (0, 1):
        forward_q(0, dc)
        forward_k(0, dc)
    forward_ld(0)
    dq[...] = jnp.zeros_like(dq)
    acc[...] = jnp.zeros_like(acc)
    for dc in (1, 0):
        forward_q(1, dc)
    forward_ld(1)
    for dc in (1, 0):
        got(kv.at[piece_z(1), :, gk, core ^ dc], a_k.at[1, dc])
    for f in (a2a_q, a2a_k):
        for dc in (1, 0):
            f(3, dc)
    arrive_q(0)
    arrive_k(0)
    for dc in (1, 0):
        forward_k(1, dc, wait=False)

    def block(zq, zk, ak, j, tiles, masked):
        if j is None:
            rows, rsl, jsl = PQ, slice(None), slice(None)
        else:
            rows, rsl, jsl = PQ // 2, pl.ds(pl.multiple_of(j * 512, 512), 512), j
        q = qd[zq, 0, jsl].reshape(rows, HD)
        do = qd[zq, 1, jsl].reshape(rows, HD)
        lrow = jnp.concatenate([lb[zq, jsl].reshape(rows, HD)] * 2, 1)
        drow = jnp.concatenate([db[zq, jsl].reshape(rows, HD)] * 2, 1)
        if masked:
            row = lax.broadcasted_iota(jnp.int32, (rows, HD), 0)
            qrow = jnp.concatenate([(row >> 2) + (row >> 7) * qstep] * 2, 1)
            qpos = prefix0 + zq * 512 + qbase + j * slice_len

        def products(k0):
            ks = pl.ds(k0, TK)
            return (jnp.dot(q, kt[zk, 0, :, ks], preferred_element_type=F32),
                    jnp.dot(do, kt[zk, 1, :, ks], preferred_element_type=F32))

        def weights(k0, s, dp):
            p = jnp.exp2(s * c2 - lrow)
            if masked:
                kid = lax.broadcasted_iota(jnp.int32, (1, TK), 1) + k0
                run = sum((kid >= i * 192).astype(jnp.int32) for i in range(1, Z))
                kpos = zk * 3072 + kbase + kid + run * kstep
                p = jnp.where(qrow >= kpos - qpos, p, 0.0)
            return p.astype(BF16), (p * (dp - drow)).astype(BF16)

        total = None
        ahead = products(tiles[0])
        for i, k0 in enumerate(tiles):
            pb, ds = weights(k0, *ahead)
            if i + 1 < len(tiles):
                ahead = products(tiles[i + 1])
            ks = pl.ds(k0, TK)
            acc[ak, 1, :, ks] += jnp.dot(qt[zq, 1, :, rsl], pb, preferred_element_type=F32)
            acc[ak, 0, :, ks] += jnp.dot(qt[zq, 0, :, rsl], ds, preferred_element_type=F32)
            r = jnp.dot(ds, kn[zk, ks], preferred_element_type=F32)
            total = r if total is None else total + r
        dq[zq, jsl] += total.reshape((2, Z, HD, HD) if j is None else (Z, HD, HD))

    ALL = (0, TK, 2 * TK)

    def cell(zq, zk, ak):
        base = zk * 3072 + kbase
        early = prefix0 + zq * 512 + qbase
        full = base + 767 + 3 * kstep <= early

        @pl.when(full)
        def _():
            block(zq, zk, ak, None, ALL, False)

        @pl.when(jnp.logical_not(full))
        def _():
            def slice_j(j, _):
                q0 = early + j * slice_len
                last = q0 + 127 + 3 * qstep
                full_j = base + 767 + 3 * kstep <= q0
                seen2 = base + 512 + 2 * kstep <= last

                @pl.when(full_j)
                def _():
                    block(zq, zk, ak, j, ALL, False)

                @pl.when(jnp.logical_and(seen2, jnp.logical_not(full_j)))
                def _():
                    block(zq, zk, ak, j, ALL, True)

                @pl.when(jnp.logical_not(seen2))
                def _():
                    def tile_t(t, _):
                        @pl.when(base + t * (TK + kstep) <= last)
                        def _():
                            block(zq, zk, ak, j, (pl.multiple_of(t * TK, TK),), True)

                        return 0

                    lax.fori_loop(0, 2, tile_t, 0)

                return 0

            lax.fori_loop(0, 2, slice_j, 0)

    h0, h1 = pl.ds(0, 96), pl.ds(96, 96)

    def k_stepA(s):
        for b in range(2):
            t = acc[s, b].T
            if b == 0:
                t = t * inv_sqrt
            for y in range(4):
                part[s, y, b] = t[y * 192:(y + 1) * 192]
        rcopy(part.at[s, kO, :, h0], rak.at[s, 0], p_send.at[0], ka.at[s, 0], dkp).start()
        rcopy(part.at[s, kO, :, h1], rak.at[s, 1], p_send.at[0], ka.at[s, 1], dkm).start()
        rcopy(part.at[s, kP, :, h1], rbk.at[s, 0, :, h1], p_send.at[0], kb.at[s], dkp).start()
        rcopy(part.at[s, kM, :, h0], rbk.at[s, 1, :, h0], p_send.at[0], kb.at[s], dkm).start()

    def k_stepB(s):
        got(rak.at[s, 0], ka.at[s, 0])
        part[s, kP, :, 0:96] = part[s, kP, :, 0:96] + rak[s, 0]
        rcopy(part.at[s, kP, :, h0], rbk.at[s, 0, :, h0], p_send.at[0], kb.at[s], dkp).start()
        got(rak.at[s, 1], ka.at[s, 1])
        part[s, kM, :, 96:192] = part[s, kM, :, 96:192] + rak[s, 1]
        rcopy(part.at[s, kM, :, h1], rbk.at[s, 1, :, h1], p_send.at[0], kb.at[s], dkm).start()

    def k_stepC(s):
        got(rbk.at[s], kb.at[s])
        outk[s] = part[s, gk] + rbk[s, 0] + rbk[s, 1]
        tz = piece_z(s)

        def send(dc):
            tc = core ^ dc
            rows = pl.ds(pl.multiple_of(tc * 96, 96), 96)
            rcopy(outk.at[s, 0, rows], dk_out.at[head], o_send.at[0], o_r.at[0], dev_z(tz, tc)).start()
            rcopy(outk.at[s, 1, rows], dv_out.at[head], o_send.at[1], o_r.at[1], dev_z(tz, tc)).start()

        send(1)

        @pl.when(s > 0)
        def _():
            send(0)

        @pl.when(s == 0)
        def _():
            rows = pl.ds(pl.multiple_of(core * 96, 96), 96)
            dk_out[head] = outk[s, 0, rows]
            dv_out[head] = outk[s, 1, rows]

    def q_stepA(s):
        z = piece_z(s)
        rcopy(dq.at[z, 0, qO], raq.at[s, 0], p_send.at[1], qa.at[s, 0], dqp).start()
        rcopy(dq.at[z, 1, qO], raq.at[s, 1], p_send.at[1], qa.at[s, 1], dqm).start()
        rcopy(dq.at[z, 1, qP], rbq.at[s, 0, 1], p_send.at[1], qb.at[s], dqp).start()
        rcopy(dq.at[z, 0, qM], rbq.at[s, 1, 0], p_send.at[1], qb.at[s], dqm).start()

    def q_stepB(s):
        z = piece_z(s)
        got(raq.at[s, 0], qa.at[s, 0])
        dq[z, 0, qP] = dq[z, 0, qP] + raq[s, 0]
        rcopy(dq.at[z, 0, qP], rbq.at[s, 0, 0], p_send.at[1], qb.at[s], dqp).start()
        got(raq.at[s, 1], qa.at[s, 1])
        dq[z, 1, qM] = dq[z, 1, qM] + raq[s, 1]
        rcopy(dq.at[z, 1, qM], rbq.at[s, 1, 1], p_send.at[1], qb.at[s], dqm).start()

    def q_stepC(s):
        z = piece_z(s)
        got(rbq.at[s], qb.at[s])
        r = (dq[z, :, gq] + rbq[s, 0] + rbq[s, 1]) * inv_sqrt
        outq[s] = r.astype(BF16).reshape(2, 2, 64, 128)

        def send(dc):
            tc = core ^ dc
            rcopy(outq.at[s, :, tc], dq_out.at[head], o_send.at[2], o_r.at[2], dev_z(z, tc)).start()

        send(1)

        @pl.when(s > 0)
        def _():
            send(0)

        @pl.when(s == 0)
        def _():
            dq_out[head] = outq[s, :, core]

    def word(digits, bits):
        v = sum(int(d) << (bits * i) for i, d in enumerate(digits))
        return jnp.int32(v - (1 << 32) if v >> 31 else v)

    def pick(table, n):
        return (word(table.replace(".", "0"), 2) >> (2 * n)) & 3

    def hit(tables, n):
        on = "".join("1" if any(t[i] != "." for t in tables) else "0" for i in range(16))
        return ((word(on, 1) >> n) & 1) == 1

    def at(table, n, f):
        @pl.when(hit([table], n))
        def _():
            f(pick(table, n))

    def both(f, last=None):
        def g(a):
            f(a, 1)
            f(a, 0)
            if last is not None:
                last(a)

        return g

    def group(parts, n):
        @pl.when(hit([t for t, _ in parts], n))
        def _():
            for t, f in parts:
                at(t, n, f)

    def step(n, _):
        group(((FORWARD_Q, both(forward_q, forward_ld)), (FORWARD_K, both(forward_k)),
               (ARRIVE_Q, arrive_q), (ARRIVE_K, arrive_k)), n)
        aq, ak = pick(QUERIES, n), pick(KEYS, n)
        cell(piece_z(aq), piece_z(ak), ak)
        group(((KC, k_stepC), (QC, q_stepC), (KB, k_stepB), (QB, q_stepB), (QA, q_stepA), (KA, k_stepA)), n)
        return 0

    lax.fori_loop(0, 16, step, 0)
    one = jnp.int32
    q_stepB(one(3))
    q_stepB(one(2))
    k_stepB(one(0))
    k_stepC(one(2))
    q_stepC(one(3))
    q_stepC(one(2))
    k_stepC(one(0))

    got(dk_out.at[0:7], o_r.at[0])
    got(dv_out.at[0:7], o_r.at[1])
    got(dq_out.at[0:7], o_r.at[2])
    sent(msg.at[0:7, pl.ds(0, 256)], a_send.at[0])
    sent(msg.at[0:7, pl.ds(256, 192)], a_send.at[1])
    sent(ld.at[0:7], a_send.at[2])
    sent(qd.at[0:3], f_send.at[0])
    sent(kv.at[0:3], f_send.at[1])
    sent(ldg.at[0:3], f_send.at[2])
    sent(part.at[0:3], p_send.at[0])
    sent(dq.at[0:3], p_send.at[1])
    sent(dk_out.at[0:7], o_send.at[0])
    sent(dv_out.at[0:7], o_send.at[1])
    sent(dq_out.at[0:7], o_send.at[2])


def solution(mesh):
    cp_size = mesh.shape['cp']
    seq_spec = P(None, 'cp', 'heads', None)
    lse_spec = P(None, 'cp', 'heads')
    kv_spec = P('cp', 'heads', None)

    def local_backward(query, attn_out, grad_out, row_lse, key_cache, value_cache):
        n_slices, rows_dev, q_heads, head_dim = query.shape
        keys_dev, kv_heads, _ = key_cache.shape
        group = q_heads // kv_heads
        grp = (n_slices, rows_dev, kv_heads, group, head_dim)
        delta = jnp.sum(grad_out.astype(F32) * attn_out.astype(F32), axis=-1)

        def by_head(a):
            return a.reshape(grp).transpose(2, 0, 1, 3, 4).reshape(kv_heads, -1, head_dim)

        def rows_by_head(a):
            return a.reshape(grp[:4]).transpose(2, 0, 1, 3).reshape(kv_heads, 1, -1)

        ld = jnp.concatenate([rows_by_head(row_lse * LOG2E), rows_by_head(delta),
                              jnp.zeros((kv_heads, 6, 128), F32)], axis=1)
        msg = jnp.concatenate([by_head(query), by_head(grad_out), key_cache.transpose(1, 0, 2),
                               value_cache.transpose(1, 0, 2)], axis=1)
        vm = pl.BlockSpec(memory_space=pltpu.VMEM)
        dma = pltpu.SemaphoreType.DMA
        shape = (n_slices, rows_dev, keys_dev, head_dim, cp_size)
        scratch = [
            pltpu.VMEM((Z, 2, 2, Z, 2, 64, HD), BF16),
            pltpu.VMEM((Z, 2, Z, 2, 96, HD), BF16),
            pltpu.VMEM((Z, PK, HD), BF16),
            pltpu.VMEM((Z, Z, 2, 8, HD), F32),
            pltpu.VMEM((Z, 2, HD, PQ), BF16),
            pltpu.VMEM((Z, 2, HD, PK), BF16),
            pltpu.VMEM((Z, 2, Z, HD, HD), F32),
            pltpu.VMEM((Z, 2, Z, HD, HD), F32),
            pltpu.VMEM((Z, 2, Z, HD, HD), F32),
            pltpu.VMEM((Z, 2, HD, PK), F32),
            pltpu.VMEM((Z, Z, 2, 192, HD), F32),
            pltpu.VMEM((Z, 2, 2, 96, HD), F32),
            pltpu.VMEM((Z, 2, 2, 192, HD), F32),
            pltpu.VMEM((Z, 2, HD, HD), F32),
            pltpu.VMEM((Z, 2, 2, HD, HD), F32),
            pltpu.VMEM((Z, 2, 192, HD), F32),
            pltpu.VMEM((Z, 2, 2, 64, HD), BF16),
            dma((3,)), dma((4, 2)), dma((4, 2)), dma((Z,)),
            dma((3,)), dma((Z,)), dma((Z,)), dma((Z,)),
            dma((4, 2)), dma((Z,)), dma((4, 2)), dma((Z,)),
            dma((2,)), dma((3,)), dma((3,)),
        ]
        dq, dk, dv = pl.pallas_call(
            functools.partial(kernel, shape),
            out_shape=[jax.ShapeDtypeStruct((8, 2, 64, 128), BF16), jax.ShapeDtypeStruct((8, 96, 128), F32),
                       jax.ShapeDtypeStruct((8, 96, 128), F32)],
            in_specs=[vm] * 2, out_specs=[vm] * 3, scratch_shapes=scratch,
            compiler_params=pltpu.CompilerParams(collective_id=0, has_side_effects=True, vmem_limit_bytes=46 * 2 ** 20),
            name="attn_bwd",
        )(msg, ld)
        dq = dq.reshape(kv_heads, n_slices, rows_dev, group, head_dim).transpose(1, 2, 0, 3, 4)
        return dq.reshape(query.shape), dk.transpose(1, 0, 2), dv.transpose(1, 0, 2)

    return jax.shard_map(local_backward, mesh=mesh, in_specs=(seq_spec, seq_spec, seq_spec, lse_spec, kv_spec, kv_spec),
                         out_specs=(seq_spec, kv_spec, kv_spec), check_vma=False)
```

profile of v0, /device:TPU:1, one launch (start us, length us, event | category | flops | bytes accessed | tf_op | source)
XLA Modules:
  0.0 72.7 jit_solution(8551959227798948562)
XLA Ops:
  0.6 0.0 copy-start
  0.6 0.0 copy-start.1
  0.7 0.1 pad.2.clone
  0.7 1.3 %multiply_reduce_fusion = f32[2,16,32]{2,1,0:T(8,128)S(1)} fusion(bf16[2,16,32,128]{3,2,1,0:T(8,128)(2,1)} %param.7, bf16[2,16,32,128]{3,2,1,0:T(8,128)(2,1)} %param.8), kind=kLoop, calls=%fused_computation.1 | loop fusion | flops 523264 | bytes 528384 | tf_op jit(solution)/shard_map/reduce_sum | solution.py:425
  2.0 0.0 copy-start.2
  2.0 0.0 copy-start.3
  2.0 0.1 copy.35
  2.1 0.1 copy.36
  2.3 0.8 %copy.33 = f32[2,16,32]{1,2,0:T(8,128)S(1)} copy(f32[2,16,32]{2,1,0:T(8,128)} %param.9) | data formatting | bytes 8192 | tf_op args[3]
  3.1 0.1 copy.34
  3.2 0.1 maximum_maximum_fusion.ld
  3.3 0.0 copy-done.1
  3.3 0.1 copy.29
  3.5 0.0 copy-done
  3.5 0.1 copy.30
  3.6 0.0 copy-done.2
  3.6 0.0 copy-done.3
  3.6 0.1 copy_bitcast_fusion
  3.7 0.1 pad_maximum_fusion.msg
  3.8 66.2 %attn_bwd.1 = (bf16[8,2,64,128]{3,2,1,0:T(8,128)(2,1)S(1)}, f32[8,96,128]{2,1,0:T(8,128)S(1)}, f32[8,96,128]{2,1,0:T(8,128)S(1)}) custom-call(bf16[8,448,128]{2,1,0:T(8,128)(2,1)S(1)} %pad_maximum_fusion.msg, f32[8,8,128]{2,1,0:T(8,128)S(1)} %maximum_maximum_fusion.ld), custom_call_target="tpu_custom_call" | custom-call | tf_op jit(solution)/shard_map/attn_bwd/pallas_call | solution.py:463
  70.0 0.8 %copy.39 = bf16[2,16,8,4,128]{4,3,2,1,0:T(4,128)(2,1)} copy(bf16[2,16,8,4,128]{4,3,1,0,2:T(4,128)(2,1)S(1)} %bitcast.28) | data formatting | bytes 524288 | tf_op jit(solution)/shard_map/transpose | solution.py:471
  70.8 1.0 %copy.40 = f32[96,8,128]{2,1,0:T(8,128)} copy(f32[96,8,128]{2,0,1:T(8,128)S(1)} %bitcast.27) | data formatting | bytes 786432
  71.8 1.0 %copy.41 = f32[96,8,128]{2,1,0:T(8,128)} copy(f32[96,8,128]{2,0,1:T(8,128)S(1)} %bitcast.26) | data formatting | bytes 786432
  (4 shorter events, 0.1 us)
Async XLA Ops:
  0.6 2.8 %copy-start = (bf16[2,16,32,128]{3,2,1,0:T(8,128)(2,1)S(1)}, bf16[2,16,32,128]{3,2,1,0:T(8,128)(2,1)}, u32[]{:S(2)}) copy-start(bf16[2,16,32,128]{3,2,1,0:T(8,128)(2,1)} %param.8) | copy-start | bytes 786436
  0.6 2.7 %copy-start.1 = (bf16[2,16,32,128]{3,2,1,0:T(8,128)(2,1)S(1)}, bf16[2,16,32,128]{3,2,1,0:T(8,128)(2,1)}, u32[]{:S(2)}) copy-start(bf16[2,16,32,128]{3,2,1,0:T(8,128)(2,1)} %param.6) | copy-start | bytes 786436
  2.0 1.6 %copy-start.2 = (bf16[96,8,128]{2,1,0:T(8,128)(2,1)S(1)}, bf16[96,8,128]{2,1,0:T(8,128)(2,1)}, u32[]{:S(2)}) copy-start(bf16[96,8,128]{2,1,0:T(8,128)(2,1)} %param.11) | copy-start | bytes 589828
  2.0 1.6 %copy-start.3 = (bf16[96,8,128]{2,1,0:T(8,128)(2,1)S(1)}, bf16[96,8,128]{2,1,0:T(8,128)(2,1)}, u32[]{:S(2)}) copy-start(bf16[96,8,128]{2,1,0:T(8,128)(2,1)} %param.10) | copy-start | bytes 589828
where the time goes:
time: 72.9 us; the launch traced here: 72.7 us
  Pallas kernels  66.2 us (91%)
  local copies, waits for them, and re-layouts  4.32 us (6%)
  other arithmetic  1.44 us (2%)
  between operations  0.76 us (1%)
    pallas_call x1, Pallas kernels, local_backward(): pl.pallas_call(functools.partial(kernel, shape), out_shape=[jax.ShapeDtyp...  66.2 us
    unnamed x11, local copies, waits for them, and re-layouts  2.79 us

commit v1 on v0

--- a/solution.py
+++ b/solution.py
@@ -32,7 +32,8 @@
 KA = ".....1...3...2.0"
 
 
-def kernel(shape, msg, ld, dq_out, dk_out, dv_out, qd, kv, kn, ldg, qt, kt, lb, db,
+def kernel(shape, query, attn_out, grad_out, row_lse, key_cache, value_cache, dq_out, dk_out, dv_out,
+           in_q, in_o, in_do, in_lse, in_k, in_v, rows32, msg, ld, in_sems, qd, kv, kn, ldg, qt, kt, lb, db,
            dq, acc, part, rak, rbk, raq, rbq, outk, outq,
            a_send, a_q, a_k, a_l, f_send, q_r, k_r, l_r,
            ka, kb, qa, qb, p_send, o_send, o_r):
@@ -74,6 +75,11 @@
         return pltpu.make_async_remote_copy(src_ref=src, dst_ref=dst, send_sem=ss, recv_sem=rs,
                                             device_id={"cp": to}, device_id_type=MESH)
 
+    inputs = [pltpu.make_async_copy(src, dst, in_sems.at[i]) for i, (src, dst) in enumerate((
+        (query, in_q), (grad_out, in_do), (key_cache, in_k), (value_cache, in_v), (attn_out, in_o), (row_lse, in_lse)))]
+    for c in inputs:
+        c.start()
+
     barrier = pltpu.get_barrier_semaphore()
     peers = [dqp, dqm, dqo, dkp, dkm, dko]
     for o in range(4):
@@ -82,6 +88,15 @@
                 peers.append(dev_z(ring(zi, o), core ^ dc))
     for p in peers:
         pl.semaphore_signal(barrier, inc=1, device_id={"cp": p}, device_id_type=MESH)
+
+    def rows_of(ref, h):
+        return ref[:, :, h].astype(F32).reshape(128, HD)
+
+    for c in inputs[:2]:
+        c.wait()
+    for h in range(8):
+        msg[h, 0:128] = rows_of(in_q, h).astype(BF16)
+        msg[h, 128:256] = rows_of(in_do, h).astype(BF16)
     pl.semaphore_wait(barrier, len(peers))
 
     def got(ref, sem):
@@ -104,22 +119,14 @@
     def a2a_q(a, dc):
         h, to, tq, _ = to_head(a, dc)
         rcopy(q_msg(h), qd.at[zi, :, :, tq, core], a_send.at[0], a_q.at[a, dc], to).start()
+
+    def a2a_ld(a, dc):
+        h, to, tq, _ = to_head(a, dc)
         rcopy(ld.at[h], ldg.at[zi, tq, core], a_send.at[2], a_l.at[a], to).start()
 
     def a2a_k(a, dc):
         h, to, _, tk = to_head(a, dc)
         rcopy(k_msg(h), kv.at[zi, :, tk, core], a_send.at[1], a_k.at[a, dc], to).start()
-
-    a2a_q(0, 1)
-    a2a_k(0, 1)
-    for f in (a2a_q, a2a_k):
-        for dc in (1, 0):
-            for a in (1, 2):
-                f(a, dc)
-
-    qd[zi, :, :, gq, core] = msg[head, 0:256].reshape(2, 2, 64, HD)
-    kv[zi, :, gk, core] = msg[head, 256:448].reshape(2, 96, HD)
-    ldg[zi, gq, core] = ld[head]
 
     def forward_q(a, dc):
         sz, sc = piece_z(a), core ^ dc
@@ -163,9 +170,42 @@
             kt[sz, b] = kv[sz, b].reshape(PK, 128).T
         kn[sz] = kv[sz, 0].reshape(PK, 128)
 
-    for dc in (0, 1):
-        forward_q(0, dc)
-        forward_k(0, dc)
+    a2a_q(0, 1)
+    for dc in (1, 0):
+        for a in (1, 2):
+            a2a_q(a, dc)
+    qd[zi, :, :, gq, core] = msg[head, 0:256].reshape(2, 2, 64, HD)
+    forward_q(0, 0)
+    for c, ref, r in ((inputs[2], in_k, 256), (inputs[3], in_v, 352)):
+        c.wait()
+        rows32[...] = ref[...].astype(F32)
+        for h in range(8):
+            msg[h, r:r + 96] = rows32[:, h, :].astype(BF16)
+    a2a_k(0, 1)
+    for dc in (1, 0):
+        for a in (1, 2):
+            a2a_k(a, dc)
+    kv[zi, :, gk, core] = msg[head, 256:448].reshape(2, 96, HD)
+    forward_k(0, 0)
+    forward_q(0, 1)
+    forward_k(0, 1)
+
+    for c in inputs[4:]:
+        c.wait()
+    row = lax.broadcasted_iota(jnp.int32, (128, HD), 0)
+    lane = lax.broadcasted_iota(jnp.int32, (128, HD), 1)
+    lse = jnp.concatenate([in_lse[...].reshape(32, 32) * LOG2E, jnp.zeros((32, 96), F32)], 1)
+    lse = jnp.broadcast_to(lse.reshape(32, 1, HD), (32, Z, HD)).reshape(128, HD)
+    ld[...] = jnp.zeros_like(ld)
+    for h in range(8):
+        one = jnp.where(lane == Z * h + (row & 3), lse, 0.0)
+        ld[h, 0:1] = jnp.sum(one.T, axis=0, keepdims=True)
+        ld[h, 1:2] = jnp.sum((rows_of(in_do, h) * rows_of(in_o, h)).T, axis=0, keepdims=True)
+    a2a_ld(0, 1)
+    for dc in (1, 0):
+        for a in (1, 2):
+            a2a_ld(a, dc)
+    ldg[zi, gq, core] = ld[head]
     forward_ld(0)
     dq[...] = jnp.zeros_like(dq)
     acc[...] = jnp.zeros_like(acc)
@@ -174,7 +214,7 @@
     forward_ld(1)
     for dc in (1, 0):
         got(kv.at[piece_z(1), :, gk, core ^ dc], a_k.at[1, dc])
-    for f in (a2a_q, a2a_k):
+    for f in (a2a_q, a2a_k, a2a_ld):
         for dc in (1, 0):
             f(3, dc)
     arrive_q(0)
@@ -330,11 +370,11 @@
         z = piece_z(s)
         got(rbq.at[s], qb.at[s])
         r = (dq[z, :, gq] + rbq[s, 0] + rbq[s, 1]) * inv_sqrt
-        outq[s] = r.astype(BF16).reshape(2, 2, 64, 128)
+        outq[s] = r.reshape(2, 2, 16, 4, HD).astype(BF16)
 
         def send(dc):
             tc = core ^ dc
-            rcopy(outq.at[s, :, tc], dq_out.at[head], o_send.at[2], o_r.at[2], dev_z(z, tc)).start()
+            rcopy(outq.at[s, :, tc], dq_out.at[:, :, head], o_send.at[2], o_r.at[2], dev_z(z, tc)).start()
 
         send(1)
 
@@ -344,7 +384,7 @@
 
         @pl.when(s == 0)
         def _():
-            dq_out[head] = outq[s, :, core]
+            dq_out[:, :, head] = outq[s, :, core]
 
     def word(digits, bits):
         v = sum(int(d) << (bits * i) for i, d in enumerate(digits))
@@ -397,7 +437,7 @@
 
     got(dk_out.at[0:7], o_r.at[0])
     got(dv_out.at[0:7], o_r.at[1])
-    got(dq_out.at[0:7], o_r.at[2])
+    got(dq_out.at[:, :, 0:7], o_r.at[2])
     sent(msg.at[0:7, pl.ds(0, 256)], a_send.at[0])
     sent(msg.at[0:7, pl.ds(256, 192)], a_send.at[1])
     sent(ld.at[0:7], a_send.at[2])
@@ -408,7 +448,19 @@
     sent(dq.at[0:3], p_send.at[1])
     sent(dk_out.at[0:7], o_send.at[0])
     sent(dv_out.at[0:7], o_send.at[1])
-    sent(dq_out.at[0:7], o_send.at[2])
+    sent(dq_out.at[:, :, 0:7], o_send.at[2])
+
+
+def store_kernel(dq, dk, dv, dq_out, dk_out, dv_out, dk_rows, dv_rows, sems):
+    copies = [pltpu.make_async_copy(dq, dq_out, sems.at[0]), pltpu.make_async_copy(dk_rows, dk_out, sems.at[1]),
+              pltpu.make_async_copy(dv_rows, dv_out, sems.at[2])]
+    copies[0].start()
+    for x, rows, c in ((dk, dk_rows, copies[1]), (dv, dv_rows, copies[2])):
+        for h in range(8):
+            rows[:, h, :] = x[h]
+        c.start()
+    for c in copies:
+        c.wait()
 
 
 def solution(mesh):
@@ -422,22 +474,20 @@
         keys_dev, kv_heads, _ = key_cache.shape
         group = q_heads // kv_heads
         grp = (n_slices, rows_dev, kv_heads, group, head_dim)
-        delta = jnp.sum(grad_out.astype(F32) * attn_out.astype(F32), axis=-1)
-
-        def by_head(a):
-            return a.reshape(grp).transpose(2, 0, 1, 3, 4).reshape(kv_heads, -1, head_dim)
-
-        def rows_by_head(a):
-            return a.reshape(grp[:4]).transpose(2, 0, 1, 3).reshape(kv_heads, 1, -1)
-
-        ld = jnp.concatenate([rows_by_head(row_lse * LOG2E), rows_by_head(delta),
-                              jnp.zeros((kv_heads, 6, 128), F32)], axis=1)
-        msg = jnp.concatenate([by_head(query), by_head(grad_out), key_cache.transpose(1, 0, 2),
-                               value_cache.transpose(1, 0, 2)], axis=1)
         vm = pl.BlockSpec(memory_space=pltpu.VMEM)
         dma = pltpu.SemaphoreType.DMA
         shape = (n_slices, rows_dev, keys_dev, head_dim, cp_size)
         scratch = [
+            pltpu.VMEM(grp, BF16),
+            pltpu.VMEM(grp, BF16),
+            pltpu.VMEM(grp, BF16),
+            pltpu.VMEM(row_lse.shape, F32),
+            pltpu.VMEM(key_cache.shape, BF16),
+            pltpu.VMEM(key_cache.shape, BF16),
+            pltpu.VMEM(key_cache.shape, F32),
+            pltpu.VMEM((8, 448, HD), BF16),
+            pltpu.VMEM((8, 8, HD), F32),
+            dma((6,)),
             pltpu.VMEM((Z, 2, 2, Z, 2, 64, HD), BF16),
             pltpu.VMEM((Z, 2, Z, 2, 96, HD), BF16),
             pltpu.VMEM((Z, PK, HD), BF16),
@@ -454,7 +504,7 @@
             pltpu.VMEM((Z, 2, HD, HD), F32),
             pltpu.VMEM((Z, 2, 2, HD, HD), F32),
             pltpu.VMEM((Z, 2, 192, HD), F32),
-            pltpu.VMEM((Z, 2, 2, 64, HD), BF16),
+            pltpu.VMEM((Z, 2, 2, 16, 4, HD), BF16),
             dma((3,)), dma((4, 2)), dma((4, 2)), dma((Z,)),
             dma((3,)), dma((Z,)), dma((Z,)), dma((Z,)),
             dma((4, 2)), dma((Z,)), dma((4, 2)), dma((Z,)),
@@ -462,14 +512,22 @@
         ]
         dq, dk, dv = pl.pallas_call(
             functools.partial(kernel, shape),
-            out_shape=[jax.ShapeDtypeStruct((8, 2, 64, 128), BF16), jax.ShapeDtypeStruct((8, 96, 128), F32),
-                       jax.ShapeDtypeStruct((8, 96, 128), F32)],
-            in_specs=[vm] * 2, out_specs=[vm] * 3, scratch_shapes=scratch,
+            out_shape=[jax.ShapeDtypeStruct(grp, BF16), jax.ShapeDtypeStruct((8, 96, HD), F32),
+                       jax.ShapeDtypeStruct((8, 96, HD), F32)],
+            in_specs=[pl.BlockSpec(memory_space=pltpu.HBM)] * 6, out_specs=[vm] * 3, scratch_shapes=scratch,
             compiler_params=pltpu.CompilerParams(collective_id=0, has_side_effects=True, vmem_limit_bytes=46 * 2 ** 20),
             name="attn_bwd",
-        )(msg, ld)
-        dq = dq.reshape(kv_heads, n_slices, rows_dev, group, head_dim).transpose(1, 2, 0, 3, 4)
-        return dq.reshape(query.shape), dk.transpose(1, 0, 2), dv.transpose(1, 0, 2)
+        )(*(pltpu.with_memory_space_constraint(a, pltpu.HBM) for a in (query.reshape(grp), attn_out.reshape(grp), grad_out.reshape(grp), row_lse, key_cache, value_cache)))
+        hbm = pl.BlockSpec(memory_space=pl.ANY)
+        dq, dk, dv = pl.pallas_call(
+            store_kernel,
+            out_shape=[jax.ShapeDtypeStruct(dq.shape, BF16), jax.ShapeDtypeStruct(key_cache.shape, F32),
+                       jax.ShapeDtypeStruct(key_cache.shape, F32)],
+            in_specs=[vm] * 3, out_specs=[hbm] * 3,
+            scratch_shapes=[pltpu.VMEM(key_cache.shape, F32), pltpu.VMEM(key_cache.shape, F32), dma((3,))],
+            compiler_params=pltpu.CompilerParams(vmem_limit_bytes=2 ** 22), name="store",
+        )(dq, dk, dv)
+        return dq.reshape(query.shape), dk, dv
 
     return jax.shard_map(local_backward, mesh=mesh, in_specs=(seq_spec, seq_spec, seq_spec, lse_spec, kv_spec, kv_spec),
                          out_specs=(seq_spec, kv_spec, kv_spec), check_vma=False)

time: 72.9 us -> 70.4 us (0.966)
  local copies, waits for them, and re-layouts: 4.32 us -> 0 us
  Pallas kernels: 66.2 us -> 69.6 us
  other arithmetic: 1.44 us -> 0 us
    unnamed x11 -> x0, local copies, waits for them, and re-layouts: 2.79 us -> none
    pallas_call x1, Pallas kernels: 66.2 us -> 68.4 us  [local_backward(): pl.pallas_call(functools.partial(kernel, shape), out_shape=[jax.ShapeDtyp...]
    reduce_sum x1 -> x0, other arithmetic: 1.28 us -> none  [local_backward(): delta = jnp.sum(grad_out.astype(F32) * attn_out.astype(F32), axis=-1)]
    pallas_call x0 -> x1, Pallas kernels: none -> 1.2 us  [local_backward(): pl.pallas_call(store_kernel, out_shape=[jax.ShapeDtypeStruct(dq.shape, BF...]
    transpose x4 -> x0, local copies, waits for them, and re-layouts: 1.04 us -> none  [the longest x1 0.79 us: local_backward(): dq.reshape(kv_heads, n_slices, rows_dev, group, head_dim)]
where the time goes in v1:
time: 70.4 us; the launch traced here: 70.2 us
  Pallas kernels  69.6 us (99%)
    pallas_call x1, Pallas kernels, local_backward(): pl.pallas_call(functools.partial(kernel, shape), out_shape=[jax.ShapeDtyp...  68.4 us

profile of v1, /device:TPU:1, one launch (start us, length us, event | category | flops | bytes accessed | tf_op | source)
XLA Modules:
  0.0 70.2 jit_solution(6181218970794544760)
XLA Ops:
  0.6 68.4 %attn_bwd.1 = (bf16[2,16,8,4,128]{4,3,2,1,0:T(4,128)(2,1)S(1)}, f32[8,96,128]{2,1,0:T(8,128)S(1)}, f32[8,96,128]{2,1,0:T(8,128)S(1)}) custom-call(bf16[2,16,8,4,128]{4,3,2,1,0:T(4,128)(2,1)} %bitcast.4, bf16[2,16,8,4,128]{4,3,2,1,0:T(4,128)(2,1)} %bitcast.5, bf16[2,16,8,4,128]{4,3,2,1,0:T(4,128)(2,1)} %bitcast.6, f32[2,16,32]{2,1,0:T(8,128)} %row_lse.1, ...), custom_call_target="tpu_custom_call" | custom-call | tf_op jit(solution)/shard_map/attn_bwd/pallas_call | solution.py:513
  69.0 1.2 %store.1 = (bf16[2,16,8,4,128]{4,3,2,1,0:T(4,128)(2,1)}, f32[96,8,128]{2,1,0:T(8,128)}, f32[96,8,128]{2,1,0:T(8,128)}) custom-call(bf16[2,16,8,4,128]{4,3,2,1,0:T(4,128)(2,1)S(1)} %get-tuple-element.9.dq, f32[8,96,128]{2,1,0:T(8,128)S(1)} %get-tuple-element.10.dk, f32[8,96,128]{2,1,0:T(8,128)S(1)} %get-tuple-element.11.dv), custom_call_target="tpu_custom_call" | custom-call | tf_op jit(solution)/shard_map/store/pallas_call | solution.py:522

commit v2 on v1

--- a/solution.py
+++ b/solution.py
@@ -16,24 +16,29 @@
 PQ = 1024
 PK = 768
 TK = 256
-
-
-QUERIES = "0101230123012332"
-KEYS = "0011113333222200"
-FORWARD_Q = ".23............."
-FORWARD_K = "...32..........."
-ARRIVE_Q = ".1..23.........."
-ARRIVE_K = "..1...3...2....."
-KC = "...........1..3."
-QC = "..............01"
-KB = "........1...3..2"
-QB = "............01.."
-QA = "..........01..32"
-KA = ".....1...3...2.0"
+KR = 96
+QR = 64
+
+
+QUERIES = "1012301230123320"
+KEYS = "0111133332222000"
+FORWARD_Q = ".3.............."
+FORWARD_K = "..3..2.........."
+ARRIVE_Q = "1..23..........."
+ARRIVE_K = ".1...3...2......"
+KC = ".............1.3"
+QC = "...............1"
+KB = ".......1...3..2."
+QB = "...........01..."
+RB = "................"
+QA = ".........01..32."
+RA = "...............0"
+KA = "....1...3...2..0"
+LAST = "qB3qB2kC2qC3rB0kB0qC2qC0kC0"
 
 
 def kernel(shape, query, attn_out, grad_out, row_lse, key_cache, value_cache, dq_out, dk_out, dv_out,
-           in_q, in_o, in_do, in_lse, in_k, in_v, rows32, msg, ld, in_sems, qd, kv, kn, ldg, qt, kt, lb, db,
+           in_q, in_o, in_do, in_lse, in_k, in_v, rows32, msg, ld, in_sems, spread, qd, kv, kn, ldg, qt, kt, lb, db,
            dq, acc, part, rak, rbk, raq, rbq, outk, outq,
            a_send, a_q, a_k, a_l, f_send, q_r, k_r, l_r,
            ka, kb, qa, qb, p_send, o_send, o_r):
@@ -65,11 +70,12 @@
     def dev_z(z, c):
         return z * 32 + yi * 8 + xi * 2 + c
 
-    def off(a):
-        return a ^ (a >> 1)
+    def off(a, c):
+        o = a ^ (a >> 1)
+        return jnp.where(c == 0, o, (Z - o) & 3)
 
     def piece_z(a):
-        return ring(zi, -off(a))
+        return ring(zi, -off(a, core))
 
     def rcopy(src, dst, ss, rs, to):
         return pltpu.make_async_remote_copy(src_ref=src, dst_ref=dst, send_sem=ss, recv_sem=rs,
@@ -90,13 +96,13 @@
         pl.semaphore_signal(barrier, inc=1, device_id={"cp": p}, device_id_type=MESH)
 
     def rows_of(ref, h):
-        return ref[:, :, h].astype(F32).reshape(128, HD)
+        return ref[:, :, h].astype(F32).reshape(HD, HD)
 
     for c in inputs[:2]:
         c.wait()
     for h in range(8):
-        msg[h, 0:128] = rows_of(in_q, h).astype(BF16)
-        msg[h, 128:256] = rows_of(in_do, h).astype(BF16)
+        msg[h, :HD] = rows_of(in_q, h).astype(BF16)
+        msg[h, HD:TK] = rows_of(in_do, h).astype(BF16)
     pl.semaphore_wait(barrier, len(peers))
 
     def got(ref, sem):
@@ -106,15 +112,16 @@
         rcopy(ref, ref, sem, l_r.at[0], me).wait_send()
 
     def to_head(a, dc):
-        tz, tc = ring(zi, off(a)), core ^ dc
+        tc = core ^ dc
+        tz = ring(zi, off(a, tc))
         tq, tk = jnp.where(tc == 0, xi, yi), jnp.where(tc == 0, yi, xi)
         return tz * 2 + tc, dev_z(tz, tc), tq, tk
 
     def q_msg(h):
-        return msg.at[h, pl.ds(0, 256)].reshape(2, 2, 64, HD)
+        return msg.at[h, pl.ds(0, TK)].reshape(2, 2, QR, HD)
 
     def k_msg(h):
-        return msg.at[h, pl.ds(256, 192)].reshape(2, 96, HD)
+        return msg.at[h, pl.ds(TK, 2 * KR)].reshape(2, KR, HD)
 
     def a2a_q(a, dc):
         h, to, tq, _ = to_head(a, dc)
@@ -133,7 +140,7 @@
         c = qd.at[sz, :, :, gq, sc]
         if not (isinstance(a, int) and a == 0 and dc == 0):
             got(c, a_q.at[a, dc])
-        for to in (dqp, dqm, dqo):
+        for to in (dqo, dqp, dqm):
             rcopy(c, c, f_send.at[0], q_r.at[a], to).start()
 
     def forward_k(a, dc, wait=True):
@@ -141,7 +148,7 @@
         c = kv.at[sz, :, gk, sc]
         if not (isinstance(a, int) and a == 0 and dc == 0) and wait:
             got(c, a_k.at[a, dc])
-        for to in (dkp, dkm, dko):
+        for to in (dko, dkp, dkm):
             rcopy(c, c, f_send.at[1], k_r.at[a], to).start()
 
     def forward_ld(a):
@@ -156,12 +163,15 @@
         got(ldg.at[sz, 0:3], l_r.at[a])
         for b in range(2):
             qt[sz, b] = qd[sz, b].reshape(PQ, 128).T
-        for x in range(4):
-            for c in range(2):
-                for ref, r in ((lb, 0), (db, 1)):
-                    t = jnp.broadcast_to(ldg[sz, x, c, r:r + 1, :], (128, 128)).T
-                    ref[sz, 0, x, pl.ds(c * 64, 64)] = t[:64]
-                    ref[sz, 1, x, pl.ds(c * 64, 64)] = t[64:]
+        t = jnp.concatenate([ldg[sz].reshape(64, HD), jnp.zeros((64, HD), F32)], 0).T
+        part_of = lax.broadcasted_iota(jnp.int32, (HD, HD), 1) >> 3
+        t = jnp.concatenate([jnp.where(part_of == i, t, 0.0) for i in range(8)], 0).astype(BF16)
+        r = jnp.dot(t, spread[...], preferred_element_type=F32)
+        for i in range(8):
+            x, rows = i // 2, pl.ds(i % 2 * 64, 64)
+            for ref, v in ((lb, r[i * HD:(i + 1) * HD, :HD]), (db, r[i * HD:(i + 1) * HD, HD:])):
+                ref[sz, 0, x, rows] = v[:64]
+                ref[sz, 1, x, rows] = v[64:]
 
     def arrive_k(a):
         sz = piece_z(a)
@@ -174,49 +184,62 @@
     for dc in (1, 0):
         for a in (1, 2):
             a2a_q(a, dc)
-    qd[zi, :, :, gq, core] = msg[head, 0:256].reshape(2, 2, 64, HD)
+    qd[zi, :, :, gq, core] = msg[head, :TK].reshape(2, 2, QR, HD)
     forward_q(0, 0)
-    for c, ref, r in ((inputs[2], in_k, 256), (inputs[3], in_v, 352)):
+    for c, ref, r in ((inputs[2], in_k, TK), (inputs[3], in_v, TK + KR)):
         c.wait()
         rows32[...] = ref[...].astype(F32)
         for h in range(8):
-            msg[h, r:r + 96] = rows32[:, h, :].astype(BF16)
+            msg[h, r:r + KR] = rows32[:, h, :].astype(BF16)
     a2a_k(0, 1)
     for dc in (1, 0):
         for a in (1, 2):
             a2a_k(a, dc)
-    kv[zi, :, gk, core] = msg[head, 256:448].reshape(2, 96, HD)
+    kv[zi, :, gk, core] = msg[head, TK:].reshape(2, KR, HD)
     forward_k(0, 0)
     forward_q(0, 1)
     forward_k(0, 1)
 
     for c in inputs[4:]:
         c.wait()
-    row = lax.broadcasted_iota(jnp.int32, (128, HD), 0)
-    lane = lax.broadcasted_iota(jnp.int32, (128, HD), 1)
+    row = lax.broadcasted_iota(jnp.int32, (HD, HD), 0)
+    lane = lax.broadcasted_iota(jnp.int32, (HD, HD), 1)
     lse = jnp.concatenate([in_lse[...].reshape(32, 32) * LOG2E, jnp.zeros((32, 96), F32)], 1)
-    lse = jnp.broadcast_to(lse.reshape(32, 1, HD), (32, Z, HD)).reshape(128, HD)
-    ld[...] = jnp.zeros_like(ld)
+    lse = jnp.broadcast_to(lse.reshape(32, 1, HD), (32, Z, HD)).reshape(HD, HD)
+    def pieces(x):
+        out = []
+        for _ in range(3):
+            out.append(x.astype(BF16).astype(F32))
+            x = x - out[-1]
+        return out
+
     for h in range(8):
         one = jnp.where(lane == Z * h + (row & 3), lse, 0.0)
-        ld[h, 0:1] = jnp.sum(one.T, axis=0, keepdims=True)
-        ld[h, 1:2] = jnp.sum((rows_of(in_do, h) * rows_of(in_o, h)).T, axis=0, keepdims=True)
+        d = rows_of(in_do, h) * rows_of(in_o, h)
+        ld[h] = jnp.concatenate([*pieces(jnp.sum(one.T, axis=0, keepdims=True)), *pieces(jnp.sum(d.T, axis=0, keepdims=True)),
+                                 jnp.zeros((2, HD), F32)], 0)
     a2a_ld(0, 1)
     for dc in (1, 0):
         for a in (1, 2):
             a2a_ld(a, dc)
     ldg[zi, gq, core] = ld[head]
     forward_ld(0)
+    kind = lax.broadcasted_iota(jnp.int32, (HD, 2 * HD), 0) & 7
+    want = (lax.broadcasted_iota(jnp.int32, (HD, 2 * HD), 1) >> 7) * 3
+    spread[...] = jnp.where(jnp.logical_and(kind >= want, kind < want + 3), 1.0, 0.0).astype(BF16)
     dq[...] = jnp.zeros_like(dq)
     acc[...] = jnp.zeros_like(acc)
     for dc in (1, 0):
         forward_q(1, dc)
     forward_ld(1)
-    for dc in (1, 0):
-        got(kv.at[piece_z(1), :, gk, core ^ dc], a_k.at[1, dc])
     for f in (a2a_q, a2a_k, a2a_ld):
         for dc in (1, 0):
             f(3, dc)
+    for dc in (1, 0):
+        forward_q(2, dc)
+    forward_ld(2)
+    for dc in (1, 0):
+        got(kv.at[piece_z(1), :, gk, core ^ dc], a_k.at[1, dc])
     arrive_q(0)
     arrive_k(0)
     for dc in (1, 0):
@@ -265,10 +288,10 @@
 
     ALL = (0, TK, 2 * TK)
 
-    def cell(zq, zk, ak):
+    def cell(zq, zk, ak, j0=0, j1=2):
         base = zk * 3072 + kbase
         early = prefix0 + zq * 512 + qbase
-        full = base + 767 + 3 * kstep <= early
+        full = jnp.logical_and(base + 767 + 3 * kstep <= early, j1 - j0 == 2)
 
         @pl.when(full)
         def _():
@@ -303,9 +326,9 @@
 
                 return 0
 
-            lax.fori_loop(0, 2, slice_j, 0)
-
-    h0, h1 = pl.ds(0, 96), pl.ds(96, 96)
+            lax.fori_loop(j0, j1, slice_j, 0)
+
+    h0, h1 = pl.ds(0, KR), pl.ds(KR, KR)
 
     def k_stepA(s):
         for b in range(2):
@@ -313,7 +336,7 @@
             if b == 0:
                 t = t * inv_sqrt
             for y in range(4):
-                part[s, y, b] = t[y * 192:(y + 1) * 192]
+                part[s, y, b] = t[y * 2 * KR:(y + 1) * 2 * KR]
         rcopy(part.at[s, kO, :, h0], rak.at[s, 0], p_send.at[0], ka.at[s, 0], dkp).start()
         rcopy(part.at[s, kO, :, h1], rak.at[s, 1], p_send.at[0], ka.at[s, 1], dkm).start()
         rcopy(part.at[s, kP, :, h1], rbk.at[s, 0, :, h1], p_send.at[0], kb.at[s], dkp).start()
@@ -321,10 +344,10 @@
 
     def k_stepB(s):
         got(rak.at[s, 0], ka.at[s, 0])
-        part[s, kP, :, 0:96] = part[s, kP, :, 0:96] + rak[s, 0]
+        part[s, kP, :, :KR] = part[s, kP, :, :KR] + rak[s, 0]
         rcopy(part.at[s, kP, :, h0], rbk.at[s, 0, :, h0], p_send.at[0], kb.at[s], dkp).start()
         got(rak.at[s, 1], ka.at[s, 1])
-        part[s, kM, :, 96:192] = part[s, kM, :, 96:192] + rak[s, 1]
+        part[s, kM, :, KR:] = part[s, kM, :, KR:] + rak[s, 1]
         rcopy(part.at[s, kM, :, h1], rbk.at[s, 1, :, h1], p_send.at[0], kb.at[s], dkm).start()
 
     def k_stepC(s):
@@ -350,21 +373,29 @@
             dk_out[head] = outk[s, 0, rows]
             dv_out[head] = outk[s, 1, rows]
 
+    def r_stepA(s):
+        z = piece_z(s)
+        rcopy(dq.at[z, 1, qO], raq.at[s, 1], p_send.at[1], qa.at[s, 1], dqm).start()
+        rcopy(dq.at[z, 1, qP], rbq.at[s, 0, 1], p_send.at[1], qb.at[s], dqp).start()
+
     def q_stepA(s):
         z = piece_z(s)
         rcopy(dq.at[z, 0, qO], raq.at[s, 0], p_send.at[1], qa.at[s, 0], dqp).start()
-        rcopy(dq.at[z, 1, qO], raq.at[s, 1], p_send.at[1], qa.at[s, 1], dqm).start()
-        rcopy(dq.at[z, 1, qP], rbq.at[s, 0, 1], p_send.at[1], qb.at[s], dqp).start()
         rcopy(dq.at[z, 0, qM], rbq.at[s, 1, 0], p_send.at[1], qb.at[s], dqm).start()
+        pl.when(s > 0)(lambda: r_stepA(s))
+
+    def r_stepB(s):
+        z = piece_z(s)
+        got(raq.at[s, 1], qa.at[s, 1])
+        dq[z, 1, qM] = dq[z, 1, qM] + raq[s, 1]
+        rcopy(dq.at[z, 1, qM], rbq.at[s, 1, 1], p_send.at[1], qb.at[s], dqm).start()
 
     def q_stepB(s):
         z = piece_z(s)
         got(raq.at[s, 0], qa.at[s, 0])
         dq[z, 0, qP] = dq[z, 0, qP] + raq[s, 0]
         rcopy(dq.at[z, 0, qP], rbq.at[s, 0, 0], p_send.at[1], qb.at[s], dqp).start()
-        got(raq.at[s, 1], qa.at[s, 1])
-        dq[z, 1, qM] = dq[z, 1, qM] + raq[s, 1]
-        rcopy(dq.at[z, 1, qM], rbq.at[s, 1, 1], p_send.at[1], qb.at[s], dqm).start()
+        pl.when(s > 0)(lambda: r_stepB(s))
 
     def q_stepC(s):
         z = piece_z(s)
@@ -421,25 +452,21 @@
         group(((FORWARD_Q, both(forward_q, forward_ld)), (FORWARD_K, both(forward_k)),
                (ARRIVE_Q, arrive_q), (ARRIVE_K, arrive_k)), n)
         aq, ak = pick(QUERIES, n), pick(KEYS, n)
-        cell(piece_z(aq), piece_z(ak), ak)
-        group(((KC, k_stepC), (QC, q_stepC), (KB, k_stepB), (QB, q_stepB), (QA, q_stepA), (KA, k_stepA)), n)
+        cell(piece_z(aq), piece_z(ak), ak, jnp.where(n == 15, 1, 0))
+        group(((KB, k_stepB), (QC, q_stepC), (QA, q_stepA), (RB, r_stepB), (KC, k_stepC), (QB, q_stepB), (RA, r_stepA), (KA, k_stepA)), n)
         return 0
 
+    cell(zi, zi, 0, 0, 1)
     lax.fori_loop(0, 16, step, 0)
-    one = jnp.int32
-    q_stepB(one(3))
-    q_stepB(one(2))
-    k_stepB(one(0))
-    k_stepC(one(2))
-    q_stepC(one(3))
-    q_stepC(one(2))
-    k_stepC(one(0))
+    steps = {"qB": q_stepB, "rB": r_stepB, "qC": q_stepC, "kB": k_stepB, "kC": k_stepC}
+    for i in range(0, len(LAST), 3):
+        steps[LAST[i:i + 2]](jnp.int32(int(LAST[i + 2])))
 
     got(dk_out.at[0:7], o_r.at[0])
     got(dv_out.at[0:7], o_r.at[1])
     got(dq_out.at[:, :, 0:7], o_r.at[2])
-    sent(msg.at[0:7, pl.ds(0, 256)], a_send.at[0])
-    sent(msg.at[0:7, pl.ds(256, 192)], a_send.at[1])
+    sent(msg.at[0:7, pl.ds(0, TK)], a_send.at[0])
+    sent(msg.at[0:7, pl.ds(TK, 2 * KR)], a_send.at[1])
     sent(ld.at[0:7], a_send.at[2])
     sent(qd.at[0:3], f_send.at[0])
     sent(kv.at[0:3], f_send.at[1])
@@ -488,8 +515,9 @@
             pltpu.VMEM((8, 448, HD), BF16),
             pltpu.VMEM((8, 8, HD), F32),
             dma((6,)),
+            pltpu.VMEM((HD, 2 * HD), BF16),
             pltpu.VMEM((Z, 2, 2, Z, 2, 64, HD), BF16),
-            pltpu.VMEM((Z, 2, Z, 2, 96, HD), BF16),
+            pltpu.VMEM((Z, 2, Z, 2, KR, HD), BF16),
             pltpu.VMEM((Z, PK, HD), BF16),
             pltpu.VMEM((Z, Z, 2, 8, HD), F32),
             pltpu.VMEM((Z, 2, HD, PQ), BF16),
@@ -498,12 +526,12 @@
             pltpu.VMEM((Z, 2, Z, HD, HD), F32),
             pltpu.VMEM((Z, 2, Z, HD, HD), F32),
             pltpu.VMEM((Z, 2, HD, PK), F32),
-            pltpu.VMEM((Z, Z, 2, 192, HD), F32),
-            pltpu.VMEM((Z, 2, 2, 96, HD), F32),
-            pltpu.VMEM((Z, 2, 2, 192, HD), F32),
+            pltpu.VMEM((Z, Z, 2, 2 * KR, HD), F32),
+            pltpu.VMEM((Z, 2, 2, KR, HD), F32),
+            pltpu.VMEM((Z, 2, 2, 2 * KR, HD), F32),
             pltpu.VMEM((Z, 2, HD, HD), F32),
             pltpu.VMEM((Z, 2, 2, HD, HD), F32),
-            pltpu.VMEM((Z, 2, 192, HD), F32),
+            pltpu.VMEM((Z, 2, 2 * KR, HD), F32),
             pltpu.VMEM((Z, 2, 2, 16, 4, HD), BF16),
             dma((3,)), dma((4, 2)), dma((4, 2)), dma((Z,)),
             dma((3,)), dma((Z,)), dma((Z,)), dma((Z,)),
@@ -512,8 +540,8 @@
         ]
         dq, dk, dv = pl.pallas_call(
             functools.partial(kernel, shape),
-            out_shape=[jax.ShapeDtypeStruct(grp, BF16), jax.ShapeDtypeStruct((8, 96, HD), F32),
-                       jax.ShapeDtypeStruct((8, 96, HD), F32)],
+            out_shape=[jax.ShapeDtypeStruct(grp, BF16), jax.ShapeDtypeStruct((8, KR, HD), F32),
+                       jax.ShapeDtypeStruct((8, KR, HD), F32)],
             in_specs=[pl.BlockSpec(memory_space=pltpu.HBM)] * 6, out_specs=[vm] * 3, scratch_shapes=scratch,
             compiler_params=pltpu.CompilerParams(collective_id=0, has_side_effects=True, vmem_limit_bytes=46 * 2 ** 20),
             name="attn_bwd",

time: 70.4 us -> 68.8 us (0.977)
  Pallas kernels: 69.6 us -> 68.1 us
    pallas_call x1, Pallas kernels: 68.4 us -> 66.9 us  [local_backward(): pl.pallas_call(functools.partial(kernel, shape), out_shape=[jax.ShapeDtyp...]
where the time goes in v2:
time: 68.8 us; the launch traced here: 68.7 us
  Pallas kernels  68.1 us (99%)
    pallas_call x1, Pallas kernels, local_backward(): pl.pallas_call(functools.partial(kernel, shape), out_shape=[jax.ShapeDtyp...  66.9 us

profile of v2, /device:TPU:1, one launch (start us, length us, event | category | flops | bytes accessed | tf_op | source)
XLA Modules:
  0.0 68.7 jit_solution(13320805343568346717)
XLA Ops:
  0.6 66.9 %attn_bwd.1 = (bf16[2,16,8,4,128]{4,3,2,1,0:T(4,128)(2,1)S(1)}, f32[8,96,128]{2,1,0:T(8,128)S(1)}, f32[8,96,128]{2,1,0:T(8,128)S(1)}) custom-call(bf16[2,16,8,4,128]{4,3,2,1,0:T(4,128)(2,1)} %bitcast.4, bf16[2,16,8,4,128]{4,3,2,1,0:T(4,128)(2,1)} %bitcast.5, bf16[2,16,8,4,128]{4,3,2,1,0:T(4,128)(2,1)} %bitcast.6, f32[2,16,32]{2,1,0:T(8,128)} %row_lse.1, ...), custom_call_target="tpu_custom_call" | custom-call | tf_op jit(solution)/shard_map/attn_bwd/pallas_call | solution.py:541
  67.5 1.2 %store.1 = (bf16[2,16,8,4,128]{4,3,2,1,0:T(4,128)(2,1)}, f32[96,8,128]{2,1,0:T(8,128)}, f32[96,8,128]{2,1,0:T(8,128)}) custom-call(bf16[2,16,8,4,128]{4,3,2,1,0:T(4,128)(2,1)S(1)} %get-tuple-element.9.dq, f32[8,96,128]{2,1,0:T(8,128)S(1)} %get-tuple-element.10.dk, f32[8,96,128]{2,1,0:T(8,128)S(1)} %get-tuple-element.11.dv), custom_call_target="tpu_custom_call" | custom-call | tf_op jit(solution)/shard_map/store/pallas_call | solution.py:550

commit v3 on v2

--- a/solution.py
+++ b/solution.py
@@ -34,7 +34,7 @@
 QA = ".........01..32."
 RA = "...............0"
 KA = "....1...3...2..0"
-LAST = "qB3qB2kC2qC3rB0kB0qC2qC0kC0"
+LAST = "qB3qB2kC2qC3kB0rB0qC2kC0qC0"
 
 
 def kernel(shape, query, attn_out, grad_out, row_lse, key_cache, value_cache, dq_out, dk_out, dv_out,
@@ -133,7 +133,7 @@
 
     def a2a_k(a, dc):
         h, to, _, tk = to_head(a, dc)
-        rcopy(k_msg(h), kv.at[zi, :, tk, core], a_send.at[1], a_k.at[a, dc], to).start()
+        rcopy(k_msg(h), kv.at[zi, :, tk, core], a_send.at[1], a_k.at[a], to).start()
 
     def forward_q(a, dc):
         sz, sc = piece_z(a), core ^ dc
@@ -146,8 +146,8 @@
     def forward_k(a, dc, wait=True):
         sz, sc = piece_z(a), core ^ dc
         c = kv.at[sz, :, gk, sc]
-        if not (isinstance(a, int) and a == 0 and dc == 0) and wait:
-            got(c, a_k.at[a, dc])
+        if dc == 1 and wait:
+            got(c if isinstance(a, int) else kv.at[sz, :, gk], a_k.at[a])
         for to in (dko, dkp, dkm):
             rcopy(c, c, f_send.at[1], k_r.at[a], to).start()
 
@@ -238,8 +238,7 @@
     for dc in (1, 0):
         forward_q(2, dc)
     forward_ld(2)
-    for dc in (1, 0):
-        got(kv.at[piece_z(1), :, gk, core ^ dc], a_k.at[1, dc])
+    got(kv.at[piece_z(1), :, gk], a_k.at[1])
     arrive_q(0)
     arrive_k(0)
     for dc in (1, 0):
@@ -533,9 +532,9 @@
             pltpu.VMEM((Z, 2, 2, HD, HD), F32),
             pltpu.VMEM((Z, 2, 2 * KR, HD), F32),
             pltpu.VMEM((Z, 2, 2, 16, 4, HD), BF16),
-            dma((3,)), dma((4, 2)), dma((4, 2)), dma((Z,)),
+            dma((3,)), dma((Z, 2)), dma((Z,)), dma((Z,)),
             dma((3,)), dma((Z,)), dma((Z,)), dma((Z,)),
-            dma((4, 2)), dma((Z,)), dma((4, 2)), dma((Z,)),
+            dma((Z, 2)), dma((Z,)), dma((Z, 2)), dma((Z,)),
             dma((2,)), dma((3,)), dma((3,)),
         ]
         dq, dk, dv = pl.pallas_call(

time: 68.8 us -> 69 us (level)
  no operation moved by 1% of the time
where the time goes in v3:
time: 69 us; the launch traced here: 68.8 us
  Pallas kernels  68.2 us (99%)
    pallas_call x1, Pallas kernels, local_backward(): pl.pallas_call(functools.partial(kernel, shape), out_shape=[jax.ShapeDtyp...  67 us

profile of v3, /device:TPU:1, one launch (start us, length us, event | category | flops | bytes accessed | tf_op | source)
XLA Modules:
  0.0 68.8 jit_solution(14934715105171996644)
XLA Ops:
  0.6 67.0 %attn_bwd.1 = (bf16[2,16,8,4,128]{4,3,2,1,0:T(4,128)(2,1)S(1)}, f32[8,96,128]{2,1,0:T(8,128)S(1)}, f32[8,96,128]{2,1,0:T(8,128)S(1)}) custom-call(bf16[2,16,8,4,128]{4,3,2,1,0:T(4,128)(2,1)} %bitcast.4, bf16[2,16,8,4,128]{4,3,2,1,0:T(4,128)(2,1)} %bitcast.5, bf16[2,16,8,4,128]{4,3,2,1,0:T(4,128)(2,1)} %bitcast.6, f32[2,16,32]{2,1,0:T(8,128)} %row_lse.1, ...), custom_call_target="tpu_custom_call" | custom-call | tf_op jit(solution)/shard_map/attn_bwd/pallas_call | solution.py:540
  67.6 1.2 %store.1 = (bf16[2,16,8,4,128]{4,3,2,1,0:T(4,128)(2,1)}, f32[96,8,128]{2,1,0:T(8,128)}, f32[96,8,128]{2,1,0:T(8,128)}) custom-call(bf16[2,16,8,4,128]{4,3,2,1,0:T(4,128)(2,1)S(1)} %get-tuple-element.9.dq, f32[8,96,128]{2,1,0:T(8,128)S(1)} %get-tuple-element.10.dk, f32[8,96,128]{2,1,0:T(8,128)S(1)} %get-tuple-element.11.dv), custom_call_target="tpu_custom_call" | custom-call | tf_op jit(solution)/shard_map/store/pallas_call | solution.py:549
